TPU v7x, 128 devices: a whole 4x4x4 slice. The times are simulated.
128 devices in a mesh: dp: 8 (over y, x_lo), tp: 16 (over z, x_hi, core).
Axes of the slice: x: 4 (x_hi: 2, x_lo: 2; x = x_hi * 2 + x_lo), y: 4, z: 4, core: 2. Of those that a mesh axis runs over, the one named last changes fastest.
Arguments:
- gradients: bfloat16 [8, 4, 3072, 768], P('dp', None, 'tp'), may hold values from -6 to 6, as said below
- right_factor: float32 [4, 768, 8], replicated, may hold values from -6 to 6
- weights_before: float32 [4, 3072, 768], P(None, 'tp', 'dp'), may hold values from -0.21875 to 0.21875
- momentum: float32 [4, 3072, 768], P(None, 'tp', 'dp'), may hold values from -0.3125 to 0.3125
Outputs:
- new_weights: float32 [4, 3072, 768], P(None, 'tp', 'dp')
- new_basis: float32 [4, 768, 8], replicated
- new_momentum: float32 [4, 3072, 768], P(None, 'tp', 'dp')
Inputs may be any that keep to these rules, and one draw needn't show every extreme that they name: gradients holds numbers from -6 to 6.
All inputs are finite; a program needn't handle non-finite values.
Results may differ from a plain program's by a relative error of at most 0.0003.
Values sent between devices are 32-bit elements.
A program may use at most 64 MiB of HBM per device.

v0:
```python
import functools

import jax
import jax.numpy as jnp
from jax import lax
from jax.experimental import pallas as pl
from jax.experimental.pallas import tpu as pltpu
from jax.sharding import PartitionSpec as P

MESH = pl.DeviceIdType.MESH
LANES = 128


def split3(x):
    high = x.astype(jnp.bfloat16).astype(jnp.float32)
    rest = x - high
    mid = rest.astype(jnp.bfloat16).astype(jnp.float32)
    low = (rest - mid).astype(jnp.bfloat16).astype(jnp.float32)
    return high, mid, low


def kernel(
    ndp, ntp, grads, basis, weights, momentum,
    out_weights, out_basis, out_momentum,
    b_buf, g_buf, w_buf, m_buf, lefts, grams, rights, parts, full, y_buf,
    g_sem, wm_sem, left_send, left_recv, gram_send, gram_recv, part_send, part_recv, full_send, full_recv,
):
    layers, rank, rows = lefts.shape[0], lefts.shape[2], lefts.shape[3]
    width = grads.shape[2]
    columns = weights.shape[1]
    n = ndp * ntp
    tiles = width // LANES
    pieces = layers * tiles
    my_dp, my_tp = lax.axis_index("dp"), lax.axis_index("tp")
    me = my_dp * ntp + my_tp

    group = -(-pieces // ndp)
    span = max(
        ((d + 1) * columns - 1) // LANES - d * columns // LANES + 1 for d in range(ndp)
    )

    def device(flat):
        return (flat // ntp, lax.rem(flat, ntp))

    def owner_of(l, t):
        place = t * layers + l
        within = place % group
        tp = within * ntp // group if group <= ntp else within % ntp
        return place // group * ntp + tp

    def round_of(l, t):
        return 0 if group <= ntp else (t * layers + l) % group // ntp

    def first_tile(d, least=min):
        return least(d * columns // LANES, tiles - span)

    loads = [pltpu.make_async_copy(grads.at[l], g_buf.at[l], g_sem.at[l]) for l in range(layers)]
    for load in loads:
        load.start()
    basis_load = pltpu.make_async_copy(basis, b_buf, wm_sem.at[2])
    basis_load.start()
    state_loads = [
        pltpu.make_async_copy(weights, w_buf, wm_sem.at[0]),
        pltpu.make_async_copy(momentum, m_buf, wm_sem.at[1]),
    ]
    for load in state_loads:
        load.start()

    grams[my_tp] = jnp.zeros(grams.shape[1:], jnp.float32)
    barrier = pltpu.get_barrier_semaphore()
    for k in range(1, n):
        pl.semaphore_signal(barrier, inc=1, device_id=device(lax.rem(me + k, n)), device_id_type=MESH)

    def left_copy(l, k):
        return pltpu.make_async_remote_copy(
            src_ref=lefts.at[l, my_dp], dst_ref=lefts.at[l, my_dp],
            send_sem=left_send, recv_sem=left_recv.at[l],
            device_id=(lax.rem(my_dp + k, ndp), my_tp), device_id_type=MESH,
        )

    for l in range(layers):
        if l == 0:
            basis_load.wait()
        loads[l].wait()
        lefts[l, my_dp] = lax.dot_general(
            b_buf[l].astype(jnp.bfloat16), g_buf[l], (((1,), (1,)), ((), ())), preferred_element_type=jnp.float32
        )
    pl.semaphore_wait(barrier, n - 1)
    for l in range(layers):
        for k in range(1, ndp):
            left_copy(l, k).start()

    def part_copy(l, t):
        j, owner, turn = l * tiles + t, owner_of(l, t), round_of(l, t)
        return pltpu.make_async_remote_copy(
            src_ref=rights.at[j], dst_ref=parts.at[turn, me],
            send_sem=part_send, recv_sem=part_recv.at[turn],
            device_id=(owner // ntp, owner % ntp), device_id_type=MESH,
        )

    all_left = []
    for l in range(layers):
        if ndp > 1:
            landed = lefts.at[l, pl.ds(0, ndp - 1)]
            pltpu.make_async_copy(landed, landed, left_recv.at[l]).wait()
        left = lefts[l, 0]
        for d in range(1, ndp):
            left = left + lefts[l, d]
        all_left.append(left)
        right = jnp.dot(left.astype(jnp.bfloat16), g_buf[l], preferred_element_type=jnp.float32)
        for t in range(tiles):
            rights[l * tiles + t] = right[:, t * LANES:(t + 1) * LANES]
        for t in range(tiles):

            @pl.when(me != owner_of(l, t))
            def _():
                part_copy(l, t).start()

    stacked = jnp.concatenate(all_left, axis=0)
    products = lax.dot_general(
        stacked, stacked, (((1,), (1,)), ((), ())),
        precision=lax.Precision.HIGHEST, preferred_element_type=jnp.float32,
    )
    where = lax.broadcasted_iota(jnp.int32, (rank, layers * rank), 1) // rank
    packed = jnp.zeros((rank, layers * rank), jnp.float32)
    for l in range(layers):
        packed = jnp.where(where == l, products[l * rank:(l + 1) * rank], packed)
    grams[my_tp, :, :layers * rank] = packed

    def gram_copy(k):
        return pltpu.make_async_remote_copy(
            src_ref=grams.at[my_tp], dst_ref=grams.at[my_tp],
            send_sem=gram_send, recv_sem=gram_recv,
            device_id=(my_dp, lax.rem(my_tp + k, ntp)), device_id_type=MESH,
        )

    for k in range(1, ntp):
        gram_copy(k).start()

    every = [(l, t) for l in range(layers) for t in range(tiles)]

    def full_copies(l, t):
        j, owner = l * tiles + t, owner_of(l, t)
        others = [(d, p) for d in range(ndp) for p in range(ntp) if d * ntp + p != owner]
        others.sort(key=lambda x: (not 0 <= t - first_tile(x[0]) < span, -abs(x[1] - owner % ntp)))
        return [
            pltpu.make_async_remote_copy(
                src_ref=full.at[j], dst_ref=full.at[j],
                send_sem=full_send, recv_sem=full_recv.at[j],
                device_id=other, device_id_type=MESH,
            )
            for other in others
        ]

    for l, t in every:
        q, j = round_of(l, t), l * tiles + t

        @pl.when(me == owner_of(l, t))
        def _():
            landed = parts.at[q, pl.ds(0, n - 1)]
            pltpu.make_async_copy(landed, landed, part_recv.at[q]).wait()
            parts[q, me] = rights[j]
            full[j] = jnp.sum(parts[q], axis=0)
            for copy in full_copies(l, t):
                copy.start()

    if ntp > 1:
        landed = grams.at[pl.ds(0, ntp - 1)]
        pltpu.make_async_copy(landed, landed, gram_recv).wait()
    gram_sum = jnp.sum(grams[...], axis=0)
    line = lax.broadcasted_iota(jnp.int32, (rank, rank), 0)
    diagonal = line == lax.broadcasted_iota(jnp.int32, (rank, rank), 1)
    step_line = lax.broadcasted_iota(jnp.int32, (rank, 1), 0)
    systems = []
    for l in range(layers):
        gram = gram_sum[:, l * rank:(l + 1) * rank]
        ridge = 0.001 * (jnp.sum(jnp.where(diagonal, gram, 0.0)) / rank)
        systems.append((gram + jnp.where(diagonal, ridge, 0.0), all_left[l]))
    for k in range(rank):
        after = []
        for gram, y in systems:
            pivot = 1.0 / gram[k:k + 1, k:k + 1]
            gram_row, y_row = gram[k:k + 1] * pivot, y[k:k + 1] * pivot
            factor = gram[:, k:k + 1]
            here = step_line == k
            after.append((
                jnp.where(here, gram_row, gram - factor * gram_row),
                jnp.where(here, y_row, y - factor * y_row),
            ))
        systems = after
    for l in range(layers):
        high, mid, low = split3(systems[l][1])
        y = jnp.concatenate([high, high, high, mid, mid, low], axis=0)
        y_buf[l] = y.astype(jnp.bfloat16)
    for load in state_loads:
        load.wait()

    def wait_full(j):
        pltpu.make_async_copy(full.at[j], full.at[j], full_recv.at[j]).wait()

    start = first_tile(my_dp, jnp.minimum)
    shift = lax.rem(span * LANES - (my_dp * columns - start * LANES), span * LANES)
    for l in range(layers):
        for i in range(span):
            t = start + i

            @pl.when(me != owner_of(l, t))
            def _():
                wait_full(l * tiles + t)
        near = jnp.concatenate([full[l * tiles + start + i] for i in range(span)], axis=1)
        own = pltpu.roll(near, shift, 1)[:, :columns]
        high, mid, low = split3(own)
        own = jnp.concatenate([high, mid, low, high, mid, high], axis=0).T.astype(jnp.bfloat16)
        change = jnp.dot(own, y_buf[l], preferred_element_type=jnp.float32) / ndp
        moved = 0.9 * m_buf[l] + change
        out_momentum[l] = moved
        out_weights[l] = w_buf[l] - 0.02 * moved

    for l in range(layers):
        for t in range(tiles):

            @pl.when((me != owner_of(l, t)) & ((t < start) | (t >= start + span)))
            def _():
                wait_full(l * tiles + t)
        right = jnp.concatenate([full[l * tiles + t] for t in range(tiles)], axis=1)
        out_basis[l] = right * lax.rsqrt(jnp.mean(right * right) + 1e-12)

    for l in range(layers):
        for k in range(1, ndp):
            left_copy(l, k).wait_send()
    for k in range(1, ntp):
        gram_copy(k).wait_send()
    for l, t in every:

        @pl.when(me != owner_of(l, t))
        def _():
            part_copy(l, t).wait_send()

        @pl.when(me == owner_of(l, t))
        def _():
            for copy in full_copies(l, t):
                copy.wait_send()


def solution(mesh):
    ndp, ntp = mesh.shape["dp"], mesh.shape["tp"]
    n = ndp * ntp

    def on_device(gradients, right_factor, weights_before, momentum):
        layers, rows, width = gradients.shape[1:]
        rank = right_factor.shape[2]
        columns = weights_before.shape[2]
        pieces = layers * (width // LANES)
        rounds = -(-(-(-pieces // ndp)) // ntp)
        basis = jnp.swapaxes(right_factor, 1, 2)
        f32 = jnp.float32
        keep = functools.partial(pltpu.with_memory_space_constraint, memory_space=pltpu.HBM)
        new_weights, new_basis, new_momentum = pl.pallas_call(
            functools.partial(kernel, ndp, ntp),
            out_shape=(
                jax.ShapeDtypeStruct((layers, columns, rows), f32),
                jax.ShapeDtypeStruct((layers, rank, width), f32),
                jax.ShapeDtypeStruct((layers, columns, rows), f32),
            ),
            in_specs=[
                pl.BlockSpec(memory_space=pltpu.HBM),
                pl.BlockSpec(memory_space=pltpu.HBM),
                pl.BlockSpec(memory_space=pltpu.HBM),
                pl.BlockSpec(memory_space=pltpu.HBM),
            ],
            out_specs=[pl.BlockSpec(memory_space=pltpu.VMEM)] * 3,
            scratch_shapes=[
                pltpu.VMEM((layers, rank, width), f32),
                pltpu.VMEM((layers, rows, width), jnp.bfloat16),
                pltpu.VMEM((layers, columns, rows), f32),
                pltpu.VMEM((layers, columns, rows), f32),
                pltpu.VMEM((layers, ndp, rank, rows), f32),
                pltpu.VMEM((ntp, rank, LANES), f32),
                pltpu.VMEM((pieces, rank, LANES), f32),
                pltpu.VMEM((rounds, n, rank, LANES), f32),
                pltpu.VMEM((pieces, rank, LANES), f32),
                pltpu.VMEM((layers, 6 * rank, rows), jnp.bfloat16),
                pltpu.SemaphoreType.DMA((layers,)),
                pltpu.SemaphoreType.DMA((3,)),
                pltpu.SemaphoreType.DMA,
                pltpu.SemaphoreType.DMA((layers,)),
                pltpu.SemaphoreType.DMA,
                pltpu.SemaphoreType.DMA,
                pltpu.SemaphoreType.DMA,
                pltpu.SemaphoreType.DMA((rounds,)),
                pltpu.SemaphoreType.DMA,
                pltpu.SemaphoreType.DMA((pieces,)),
            ],
            compiler_params=pltpu.CompilerParams(
                collective_id=0, has_side_effects=True, vmem_limit_bytes=24 * 1024 * 1024
            ),
        )(
            keep(gradients[0]), keep(basis),
            keep(jnp.swapaxes(weights_before, 1, 2)), keep(jnp.swapaxes(momentum, 1, 2)),
        )
        return tuple(jnp.swapaxes(x, 1, 2) for x in (new_weights, new_basis, new_momentum))

    in_specs = (P("dp", None, "tp", None), P(), P(None, "tp", "dp"), P(None, "tp", "dp"))
    out_specs = (P(None, "tp", "dp"), P(), P(None, "tp", "dp"))
    return jax.shard_map(on_device, mesh=mesh, in_specs=in_specs, out_specs=out_specs, check_vma=False)
```

profile of v0, /device:TPU:1, one launch (start us, length us, event | category | flops | bytes accessed | tf_op | source)
XLA Modules:
  0.0 37.4 jit_solution(14732828330277214700)
XLA Ops:
  0.6 1.9 %copy.7 = f32[4,192,96]{1,2,0:T(8,128)} copy(f32[4,192,96]{2,1,0:T(8,128)} %param.6) | data formatting | bytes 589824 | tf_op args[2]
  2.6 1.9 %copy.8 = f32[4,192,96]{1,2,0:T(8,128)} copy(f32[4,192,96]{2,1,0:T(8,128)} %param.7) | data formatting | bytes 589824 | tf_op args[3]
  4.5 30.4 %shard_map.67 = (f32[4,96,192]{2,1,0:T(8,128)S(1)}, f32[4,8,768]{2,1,0:T(8,128)S(1)}, f32[4,96,192]{2,1,0:T(8,128)S(1)}) custom-call(bf16[4,192,768]{2,1,0:T(8,128)(2,1)} %bitcast.12, f32[4,8,768]{2,1,0:T(8,128)} %bitcast.13, f32[4,96,192]{2,1,0:T(8,128)} %bitcast.10, f32[4,96,192]{2,1,0:T(8,128)} %bitcast.11), custom_call_target="tpu_custom_call" | custom-call | tf_op jit(solution)/shard_map/pallas_call | solution.py:258
  34.9 0.9 %copy.9 = f32[4,192,96]{2,1,0:T(8,128)} copy(f32[4,192,96]{1,2,0:T(8,128)S(1)} %bitcast.8) | data formatting | bytes 589824
  35.8 0.9 %copy.10 = f32[4,192,96]{2,1,0:T(8,128)} copy(f32[4,192,96]{1,2,0:T(8,128)S(1)} %bitcast.7) | data formatting | bytes 589824
  36.7 0.6 %copy.12 = f32[4,768,8]{1,2,0:T(8,128)} copy(f32[4,768,8]{1,2,0:T(8,128)S(1)} %bitcast.9) | data formatting | bytes 196608
where the time goes:
time: 37.6 us; the launch traced here: 37.4 us
  Pallas kernels  30.4 us (81%)
  local copies, waits for them, and re-layouts  6.38 us (17%)
  between operations  0.64 us (2%)
    pallas_call x1, Pallas kernels, on_device(): pl.pallas_call(functools.partial(kernel, ndp, ntp), out_shape=(jax.ShapeD...  30.4 us
    unnamed x5, local copies, waits for them, and re-layouts  6.38 us

commit v1 on v0

--- a/solution.py
+++ b/solution.py
@@ -27,7 +27,7 @@
 ):
     layers, rank, rows = lefts.shape[0], lefts.shape[2], lefts.shape[3]
     width = grads.shape[2]
-    columns = weights.shape[1]
+    columns = weights.shape[2]
     n = ndp * ntp
     tiles = width // LANES
     pieces = layers * tiles
@@ -189,9 +189,9 @@
             ))
         systems = after
     for l in range(layers):
-        high, mid, low = split3(systems[l][1])
+        high, mid, low = split3(systems[l][1] / ndp)
         y = jnp.concatenate([high, high, high, mid, mid, low], axis=0)
-        y_buf[l] = y.astype(jnp.bfloat16)
+        y_buf[l] = y.T.astype(jnp.bfloat16)
     for load in state_loads:
         load.wait()
 
@@ -210,8 +210,8 @@
         near = jnp.concatenate([full[l * tiles + start + i] for i in range(span)], axis=1)
         own = pltpu.roll(near, shift, 1)[:, :columns]
         high, mid, low = split3(own)
-        own = jnp.concatenate([high, mid, low, high, mid, high], axis=0).T.astype(jnp.bfloat16)
-        change = jnp.dot(own, y_buf[l], preferred_element_type=jnp.float32) / ndp
+        own = jnp.concatenate([high, mid, low, high, mid, high], axis=0).astype(jnp.bfloat16)
+        change = jnp.dot(y_buf[l], own, preferred_element_type=jnp.float32)
         moved = 0.9 * m_buf[l] + change
         out_momentum[l] = moved
         out_weights[l] = w_buf[l] - 0.02 * moved
@@ -240,6 +240,15 @@
         def _():
             for copy in full_copies(l, t):
                 copy.wait_send()
+
+
+def writer(*refs):
+    half = (len(refs) - 1) // 2
+    copies = [pltpu.make_async_copy(refs[i], refs[half + i], refs[-1].at[i]) for i in range(half)]
+    for copy in copies:
+        copy.start()
+    for copy in copies:
+        copy.wait()
 
 
 def solution(mesh):
@@ -255,12 +264,12 @@
         basis = jnp.swapaxes(right_factor, 1, 2)
         f32 = jnp.float32
         keep = functools.partial(pltpu.with_memory_space_constraint, memory_space=pltpu.HBM)
-        new_weights, new_basis, new_momentum = pl.pallas_call(
+        results = pl.pallas_call(
             functools.partial(kernel, ndp, ntp),
             out_shape=(
-                jax.ShapeDtypeStruct((layers, columns, rows), f32),
+                jax.ShapeDtypeStruct((layers, rows, columns), f32),
                 jax.ShapeDtypeStruct((layers, rank, width), f32),
-                jax.ShapeDtypeStruct((layers, columns, rows), f32),
+                jax.ShapeDtypeStruct((layers, rows, columns), f32),
             ),
             in_specs=[
                 pl.BlockSpec(memory_space=pltpu.HBM),
@@ -272,14 +281,14 @@
             scratch_shapes=[
                 pltpu.VMEM((layers, rank, width), f32),
                 pltpu.VMEM((layers, rows, width), jnp.bfloat16),
-                pltpu.VMEM((layers, columns, rows), f32),
-                pltpu.VMEM((layers, columns, rows), f32),
+                pltpu.VMEM((layers, rows, columns), f32),
+                pltpu.VMEM((layers, rows, columns), f32),
                 pltpu.VMEM((layers, ndp, rank, rows), f32),
                 pltpu.VMEM((ntp, rank, LANES), f32),
                 pltpu.VMEM((pieces, rank, LANES), f32),
                 pltpu.VMEM((rounds, n, rank, LANES), f32),
                 pltpu.VMEM((pieces, rank, LANES), f32),
-                pltpu.VMEM((layers, 6 * rank, rows), jnp.bfloat16),
+                pltpu.VMEM((layers, rows, 6 * rank), jnp.bfloat16),
                 pltpu.SemaphoreType.DMA((layers,)),
                 pltpu.SemaphoreType.DMA((3,)),
                 pltpu.SemaphoreType.DMA,
@@ -296,9 +305,16 @@
             ),
         )(
             keep(gradients[0]), keep(basis),
-            keep(jnp.swapaxes(weights_before, 1, 2)), keep(jnp.swapaxes(momentum, 1, 2)),
-        )
-        return tuple(jnp.swapaxes(x, 1, 2) for x in (new_weights, new_basis, new_momentum))
+            keep(weights_before), keep(momentum),
+        )
+        new_weights, new_basis, new_momentum = pl.pallas_call(
+            writer,
+            out_shape=tuple(jax.ShapeDtypeStruct(x.shape, x.dtype) for x in results),
+            in_specs=[pl.BlockSpec(memory_space=pltpu.VMEM)] * 3,
+            out_specs=[pl.BlockSpec(memory_space=pltpu.HBM)] * 3,
+            scratch_shapes=[pltpu.SemaphoreType.DMA((3,))],
+        )(*(pltpu.with_memory_space_constraint(x, pltpu.VMEM) for x in results))
+        return new_weights, jnp.swapaxes(new_basis, 1, 2), new_momentum
 
     in_specs = (P("dp", None, "tp", None), P(), P(None, "tp", "dp"), P(None, "tp", "dp"))
     out_specs = (P(None, "tp", "dp"), P(), P(None, "tp", "dp"))

time: 37.6 us -> 32.2 us (0.86)
  local copies, waits for them, and re-layouts: 6.38 us -> 0 us
  Pallas kernels: 30.4 us -> 31.5 us
    unnamed x5 -> x0, local copies, waits for them, and re-layouts: 6.38 us -> none
    pallas_call x0 -> x1, Pallas kernels: none -> 0.94 us  [on_device(): pl.pallas_call(writer, out_shape=tuple((jax.ShapeDtypeStruct(x.shape, x.d...]
where the time goes in v1:
time: 32.2 us; the launch traced here: 32.1 us
  Pallas kernels  31.5 us (98%)
  between operations  0.64 us (2%)
    pallas_call x1, Pallas kernels, on_device(): pl.pallas_call(functools.partial(kernel, ndp, ntp), out_shape=(jax.ShapeD...  30.5 us
    pallas_call x1, Pallas kernels, on_device(): pl.pallas_call(writer, out_shape=tuple((jax.ShapeDtypeStruct(x.shape, x.d...  0.94 us

profile of v1, /device:TPU:1, one launch (start us, length us, event | category | flops | bytes accessed | tf_op | source)
XLA Modules:
  0.0 32.1 jit_solution(6338669430988796009)
XLA Ops:
  0.6 30.5 %shard_map.67 = (f32[4,192,96]{2,1,0:T(8,128)S(1)}, f32[4,8,768]{2,1,0:T(8,128)S(1)}, f32[4,192,96]{2,1,0:T(8,128)S(1)}) custom-call(bf16[4,192,768]{2,1,0:T(8,128)(2,1)} %bitcast.3, f32[4,8,768]{2,1,0:T(8,128)} %bitcast.4, f32[4,192,96]{2,1,0:T(8,128)} %weights.1, f32[4,192,96]{2,1,0:T(8,128)} %momentum.1), custom_call_target="tpu_custom_call" | custom-call | tf_op jit(solution)/shard_map/pallas_call | solution.py:267
  31.2 0.9 %shard_map.68 = (f32[4,192,96]{2,1,0:T(8,128)}, f32[4,8,768]{2,1,0:T(8,128)}, f32[4,192,96]{2,1,0:T(8,128)}) custom-call(f32[4,192,96]{2,1,0:T(8,128)S(1)} %get-tuple-element.9.refs_0_, f32[4,8,768]{2,1,0:T(8,128)S(1)} %get-tuple-element.10.refs_1_, f32[4,192,96]{2,1,0:T(8,128)S(1)} %get-tuple-element.11.refs_2_), custom_call_target="tpu_custom_call" | custom-call | tf_op jit(solution)/shard_map/pallas_call | solution.py:310

commit v2 on v1

v2 whole, which is shorter than its diff:
```python
import functools

import jax
import jax.numpy as jnp
from jax import lax
from jax.experimental import pallas as pl
from jax.experimental.pallas import tpu as pltpu
from jax.sharding import PartitionSpec as P

MESH = pl.DeviceIdType.MESH
LANES = 128


def split3(x):
    high = x.astype(jnp.bfloat16).astype(jnp.float32)
    rest = x - high
    mid = rest.astype(jnp.bfloat16).astype(jnp.float32)
    low = (rest - mid).astype(jnp.bfloat16).astype(jnp.float32)
    return high, mid, low


def pack(pair):
    whole = pair[0].shape[1] // LANES * LANES
    return jnp.concatenate([x[:, :whole] for x in pair] + [x[:, whole:] for x in pair], axis=1)


def unpack(x):
    rows = x.shape[1] // 2
    whole = rows // LANES * LANES
    rest = rows - whole
    return [
        jnp.concatenate(
            [x[:, i * whole:(i + 1) * whole], x[:, 2 * whole + i * rest:2 * whole + (i + 1) * rest]], axis=1
        )
        for i in range(2)
    ]


def owner_place(j):
    x_hi, y, z = j % 2, j // 2 % 4, j // 8
    return y * 2 + (y + z) % 2, z * 4 + x_hi * 2 + 1


def start_order(device):
    dp, tp = device
    x, y, z, core = tp // 2 % 2 * 2 + dp % 2, dp // 2, tp // 4, tp % 2
    return 10 * z + 6 * y + 4 * x + 5 * (1 - core)


def kernel(
    ndp, ntp, grads, basis, weights, momentum,
    out_weights, out_basis, out_momentum,
    b_buf, g_buf, w_buf, m_buf, lefts, grams, rights, parts, full, y_buf,
    g_sem, wm_sem, left_send, left_recv, gram_send, gram_recv, part_send, part_recv, full_send, full_recv,
):
    layers, rows, width = grads.shape
    rank = basis.shape[1]
    columns = weights.shape[2]
    n = ndp * ntp
    tiles = width // LANES
    pieces = layers * tiles
    my_dp, my_tp = lax.axis_index("dp"), lax.axis_index("tp")
    me = my_dp * ntp + my_tp

    span = max(
        ((d + 1) * columns - 1) // LANES - d * columns // LANES + 1 for d in range(ndp)
    )

    def first_tile(d, least=min):
        return least(d * columns // LANES, tiles - span)

    owners = [owner_place(j) for j in range(pieces)]
    devices = sorted(((d, p) for d in range(ndp) for p in range(ntp)), key=start_order)
    my_y, my_z = my_dp // 2, my_tp // 4
    owning = (
        (lax.rem(my_tp, 2) == 1) & (my_z * 8 < pieces) & (lax.rem(my_dp, 2) == lax.rem(my_y + my_z, 2))
    )
    my_piece = lax.min(my_z * 8 + my_y * 2 + lax.rem(my_tp // 2, 2), pieces - 1)
    my_layer = my_piece // tiles

    def is_me(device):
        return me == device[0] * ntp + device[1]

    def each_other(act):
        for device in devices:
            if device in owners:

                @pl.when(jnp.logical_not(is_me(device)))
                def _():
                    act(device)
            else:
                act(device)

    basis_load = pltpu.make_async_copy(basis, b_buf, wm_sem.at[2])
    basis_load.start()
    loads = [pltpu.make_async_copy(grads.at[l], g_buf.at[l], g_sem.at[l]) for l in range(layers)]
    for load in loads:
        load.start()
    state_loads = [
        pltpu.make_async_copy(weights, w_buf, wm_sem.at[0]),
        pltpu.make_async_copy(momentum, m_buf, wm_sem.at[1]),
    ]
    for load in state_loads:
        load.start()

    barrier = pltpu.get_barrier_semaphore()
    dp_peers = [(lax.rem(my_dp + k, ndp), my_tp) for k in range(1, ndp)]
    tp_peers = [(my_dp, lax.rem(my_tp + k, ntp)) for k in range(1, ntp)]
    for peer in dp_peers + tp_peers:
        pl.semaphore_signal(barrier, inc=1, device_id=peer, device_id_type=MESH)

    @pl.when(owning)
    def _():
        each_other(lambda device: pl.semaphore_signal(barrier, inc=1, device_id=device, device_id_type=MESH))

    grams[my_tp] = jnp.zeros(grams.shape[1:], jnp.float32)

    def left_copy(q, peer):
        return pltpu.make_async_remote_copy(
            src_ref=lefts.at[q, my_dp], dst_ref=lefts.at[q, my_dp],
            send_sem=left_send, recv_sem=left_recv.at[q],
            device_id=peer, device_id_type=MESH,
        )

    basis_load.wait()
    for load in loads:
        load.wait()
    own_left = [
        lax.dot_general(
            b_buf[l].astype(jnp.bfloat16), g_buf[l], (((1,), (1,)), ((), ())), preferred_element_type=jnp.float32
        )
        for l in range(layers)
    ]
    for q in range(layers // 2):
        lefts[q, my_dp] = pack(own_left[2 * q:2 * q + 2])
    pl.semaphore_wait(barrier, ndp - 1 + ntp - 1 + pieces - jnp.where(owning, 1, 0))
    for q in range(layers // 2):
        for peer in dp_peers:
            left_copy(q, peer).start()

    def part_copy(j):
        return pltpu.make_async_remote_copy(
            src_ref=rights.at[j], dst_ref=parts.at[me],
            send_sem=part_send, recv_sem=part_recv,
            device_id=owners[j], device_id_type=MESH,
        )

    all_left = []
    for q in range(layers // 2):
        landed = lefts.at[q, pl.ds(0, ndp - 1)]
        pltpu.make_async_copy(landed, landed, left_recv.at[q]).wait()
        both = lefts[q, 0]
        for d in range(1, ndp):
            both = both + lefts[q, d]
        for l, left in zip((2 * q, 2 * q + 1), unpack(both)):
            all_left.append(left)
            right = jnp.dot(left.astype(jnp.bfloat16), g_buf[l], preferred_element_type=jnp.float32)
            for t in range(tiles):
                rights[l * tiles + t] = right[:, t * LANES:(t + 1) * LANES]
        for j in range(2 * q * tiles, (2 * q + 2) * tiles):

            @pl.when(jnp.logical_not(is_me(owners[j])))
            def _():
                part_copy(j).start()

    stacked = jnp.concatenate(all_left, axis=0)
    products = lax.dot_general(
        stacked, stacked, (((1,), (1,)), ((), ())),
        precision=lax.Precision.HIGHEST, preferred_element_type=jnp.float32,
    )
    where = lax.broadcasted_iota(jnp.int32, (rank, layers * rank), 1) // rank
    packed = jnp.zeros((rank, layers * rank), jnp.float32)
    for l in range(layers):
        packed = jnp.where(where == l, products[l * rank:(l + 1) * rank], packed)
    grams[my_tp, :, :layers * rank] = packed

    def gram_copy(peer):
        return pltpu.make_async_remote_copy(
            src_ref=grams.at[my_tp], dst_ref=grams.at[my_tp],
            send_sem=gram_send, recv_sem=gram_recv,
            device_id=peer, device_id_type=MESH,
        )

    for peer in tp_peers:
        gram_copy(peer).start()

    def full_copy(device):
        return pltpu.make_async_remote_copy(
            src_ref=full.at[my_piece], dst_ref=full.at[my_piece],
            send_sem=full_send, recv_sem=full_recv.at[my_layer],
            device_id=device, device_id_type=MESH,
        )

    @pl.when(owning)
    def _():
        landed = parts.at[pl.ds(0, n - 1)]
        pltpu.make_async_copy(landed, landed, part_recv).wait()
        parts[me] = rights[my_piece]
        sums = [parts[i] for i in range(8)]
        for i in range(8, n):
            sums[i % 8] = sums[i % 8] + parts[i]
        while len(sums) > 1:
            sums = [a + b for a, b in zip(sums[::2], sums[1::2])]
        full[my_piece] = sums[0]
        each_other(lambda device: full_copy(device).start())

    landed_grams = grams.at[pl.ds(0, ntp - 1)]
    pltpu.make_async_copy(landed_grams, landed_grams, gram_recv).wait()
    gram_sum = jnp.sum(grams[...], axis=0)
    line = lax.broadcasted_iota(jnp.int32, (rank, rank), 0)
    diagonal = line == lax.broadcasted_iota(jnp.int32, (rank, rank), 1)
    step_line = lax.broadcasted_iota(jnp.int32, (rank, 1), 0)
    systems = []
    for l in range(layers):
        gram = gram_sum[:, l * rank:(l + 1) * rank]
        ridge = 0.001 * (jnp.sum(jnp.where(diagonal, gram, 0.0)) / rank)
        systems.append((gram + jnp.where(diagonal, ridge, 0.0), all_left[l]))
    for k in range(rank):
        after = []
        for gram, y in systems:
            pivot = 1.0 / gram[k:k + 1, k:k + 1]
            gram_row, y_row = gram[k:k + 1] * pivot, y[k:k + 1] * pivot
            factor = gram[:, k:k + 1]
            here = step_line == k
            after.append((
                jnp.where(here, gram_row, gram - factor * gram_row),
                jnp.where(here, y_row, y - factor * y_row),
            ))
        systems = after
    for l in range(layers):
        high, mid, low = split3(systems[l][1] / ndp)
        y = jnp.concatenate([high, high, high, mid, mid, low], axis=0)
        y_buf[l] = y.T.astype(jnp.bfloat16)
    for load in state_loads:
        load.wait()

    start = first_tile(my_dp, jnp.minimum)
    shift = lax.rem(span * LANES - (my_dp * columns - start * LANES), span * LANES)

    def wait_full(l, count):
        landed = full.at[pl.ds(l * tiles, count)]
        pltpu.make_async_copy(landed, landed, full_recv.at[l]).wait()

    for l in range(layers):
        own_layer = owning & (my_layer == l)

        @pl.when(own_layer)
        def _():
            wait_full(l, tiles - 1)

        @pl.when(jnp.logical_not(own_layer))
        def _():
            wait_full(l, tiles)

        near = jnp.concatenate([full[l * tiles + start + i] for i in range(span)], axis=1)
        own = pltpu.roll(near, shift, 1)[:, :columns]
        high, mid, low = split3(own)
        own = jnp.concatenate([high, mid, low, high, mid, high], axis=0).astype(jnp.bfloat16)
        change = jnp.dot(y_buf[l], own, preferred_element_type=jnp.float32)
        moved = 0.9 * m_buf[l] + change
        out_momentum[l] = moved
        out_weights[l] = w_buf[l] - 0.02 * moved
        right = jnp.concatenate([full[l * tiles + t] for t in range(tiles)], axis=1)
        out_basis[l] = right * lax.rsqrt(jnp.mean(right * right) + 1e-12)

    for q in range(layers // 2):
        sent = lefts.at[q, pl.ds(0, ndp - 1)]
        pltpu.make_async_copy(sent, sent, left_send).wait()
    pltpu.make_async_copy(landed_grams, landed_grams, gram_send).wait()

    @pl.when(owning)
    def _():
        sent = rights.at[pl.ds(0, pieces - 1)]
        pltpu.make_async_copy(sent, sent, part_send).wait()
        sent = parts.at[pl.ds(0, n - 1)]
        pltpu.make_async_copy(sent, sent, full_send).wait()

    @pl.when(jnp.logical_not(owning))
    def _():
        sent = rights.at[pl.ds(0, pieces)]
        pltpu.make_async_copy(sent, sent, part_send).wait()


def writer(*refs):
    half = (len(refs) - 1) // 2
    copies = [pltpu.make_async_copy(refs[i], refs[half + i], refs[-1].at[i]) for i in range(half)]
    for copy in copies:
        copy.start()
    for copy in copies:
        copy.wait()


def solution(mesh):
    ndp, ntp = mesh.shape["dp"], mesh.shape["tp"]
    n = ndp * ntp

    def on_device(gradients, right_factor, weights_before, momentum):
        layers, rows, width = gradients.shape[1:]
        rank = right_factor.shape[2]
        columns = weights_before.shape[2]
        pieces = layers * (width // LANES)
        basis = jnp.swapaxes(right_factor, 1, 2)
        f32 = jnp.float32
        keep = functools.partial(pltpu.with_memory_space_constraint, memory_space=pltpu.HBM)
        results = pl.pallas_call(
            functools.partial(kernel, ndp, ntp),
            out_shape=(
                jax.ShapeDtypeStruct((layers, rows, columns), f32),
                jax.ShapeDtypeStruct((layers, rank, width), f32),
                jax.ShapeDtypeStruct((layers, rows, columns), f32),
            ),
            in_specs=[
                pl.BlockSpec(memory_space=pltpu.HBM),
                pl.BlockSpec(memory_space=pltpu.HBM),
                pl.BlockSpec(memory_space=pltpu.HBM),
                pl.BlockSpec(memory_space=pltpu.HBM),
            ],
            out_specs=[pl.BlockSpec(memory_space=pltpu.VMEM)] * 3,
            scratch_shapes=[
                pltpu.VMEM((layers, rank, width), f32),
                pltpu.VMEM((layers, rows, width), jnp.bfloat16),
                pltpu.VMEM((layers, rows, columns), f32),
                pltpu.VMEM((layers, rows, columns), f32),
                pltpu.VMEM((layers // 2, ndp, rank, 2 * rows), f32),
                pltpu.VMEM((ntp, rank, LANES), f32),
                pltpu.VMEM((pieces, rank, LANES), f32),
                pltpu.VMEM((n, rank, LANES), f32),
                pltpu.VMEM((pieces, rank, LANES), f32),
                pltpu.VMEM((layers, rows, 6 * rank), jnp.bfloat16),
                pltpu.SemaphoreType.DMA((layers,)),
                pltpu.SemaphoreType.DMA((3,)),
                pltpu.SemaphoreType.DMA,
                pltpu.SemaphoreType.DMA((layers // 2,)),
                pltpu.SemaphoreType.DMA,
                pltpu.SemaphoreType.DMA,
                pltpu.SemaphoreType.DMA,
                pltpu.SemaphoreType.DMA,
                pltpu.SemaphoreType.DMA,
                pltpu.SemaphoreType.DMA((layers,)),
            ],
            compiler_params=pltpu.CompilerParams(
                collective_id=0, has_side_effects=True, vmem_limit_bytes=24 * 1024 * 1024
            ),
        )(
            keep(gradients[0]), keep(basis),
            keep(weights_before), keep(momentum),
        )
        new_weights, new_basis, new_momentum = pl.pallas_call(
            writer,
            out_shape=tuple(jax.ShapeDtypeStruct(x.shape, x.dtype) for x in results),
            in_specs=[pl.BlockSpec(memory_space=pltpu.VMEM)] * 3,
            out_specs=[pl.BlockSpec(memory_space=pltpu.HBM)] * 3,
            scratch_shapes=[pltpu.SemaphoreType.DMA((3,))],
        )(*(pltpu.with_memory_space_constraint(x, pltpu.VMEM) for x in results))
        return new_weights, jnp.swapaxes(new_basis, 1, 2), new_momentum

    in_specs = (P("dp", None, "tp", None), P(), P(None, "tp", "dp"), P(None, "tp", "dp"))
    out_specs = (P(None, "tp", "dp"), P(), P(None, "tp", "dp"))
    return jax.shard_map(on_device, mesh=mesh, in_specs=in_specs, out_specs=out_specs, check_vma=False)
```

time: 32.2 us -> 27.6 us (0.86)
  Pallas kernels: 31.5 us -> 26.9 us
    pallas_call x1, Pallas kernels: 30.5 us -> 25.9 us  [on_device(): pl.pallas_call(functools.partial(kernel, ndp, ntp), out_shape=(jax.ShapeD...]
where the time goes in v2:
time: 27.6 us; the launch traced here: 27.5 us
  Pallas kernels  26.9 us (97%)
  between operations  0.64 us (2%)
    pallas_call x1, Pallas kernels, on_device(): pl.pallas_call(functools.partial(kernel, ndp, ntp), out_shape=(jax.ShapeD...  25.9 us
    pallas_call x1, Pallas kernels, on_device(): pl.pallas_call(writer, out_shape=tuple((jax.ShapeDtypeStruct(x.shape, x.d...  0.94 us

profile of v2, /device:TPU:1, one launch (start us, length us, event | category | flops | bytes accessed | tf_op | source)
XLA Modules:
  0.0 27.5 jit_solution(6760855366424326257)
XLA Ops:
  0.6 25.9 %shard_map.67 = (f32[4,192,96]{2,1,0:T(8,128)S(1)}, f32[4,8,768]{2,1,0:T(8,128)S(1)}, f32[4,192,96]{2,1,0:T(8,128)S(1)}) custom-call(bf16[4,192,768]{2,1,0:T(8,128)(2,1)} %bitcast.3, f32[4,8,768]{2,1,0:T(8,128)} %bitcast.4, f32[4,192,96]{2,1,0:T(8,128)} %weights.1, f32[4,192,96]{2,1,0:T(8,128)} %momentum.1), custom_call_target="tpu_custom_call" | custom-call | tf_op jit(solution)/shard_map/pallas_call | solution.py:305
  26.6 0.9 %shard_map.68 = (f32[4,192,96]{2,1,0:T(8,128)}, f32[4,8,768]{2,1,0:T(8,128)}, f32[4,192,96]{2,1,0:T(8,128)}) custom-call(f32[4,192,96]{2,1,0:T(8,128)S(1)} %get-tuple-element.9.refs_0_, f32[4,8,768]{2,1,0:T(8,128)S(1)} %get-tuple-element.10.refs_1_, f32[4,192,96]{2,1,0:T(8,128)S(1)} %get-tuple-element.11.refs_2_), custom_call_target="tpu_custom_call" | custom-call | tf_op jit(solution)/shard_map/pallas_call | solution.py:348

commit v3 on v2

--- a/solution.py
+++ b/solution.py
@@ -52,6 +52,7 @@
     out_weights, out_basis, out_momentum,
     b_buf, g_buf, w_buf, m_buf, lefts, grams, rights, parts, full, y_buf,
     g_sem, wm_sem, left_send, left_recv, gram_send, gram_recv, part_send, part_recv, full_send, full_recv,
+    ready, go,
 ):
     layers, rows, width = grads.shape
     rank = basis.shape[1]
@@ -71,19 +72,21 @@
 
     owners = [owner_place(j) for j in range(pieces)]
     devices = sorted(((d, p) for d in range(ndp) for p in range(ntp)), key=start_order)
-    my_y, my_z = my_dp // 2, my_tp // 4
-    owning = (
-        (lax.rem(my_tp, 2) == 1) & (my_z * 8 < pieces) & (lax.rem(my_dp, 2) == lax.rem(my_y + my_z, 2))
-    )
-    my_piece = lax.min(my_z * 8 + my_y * 2 + lax.rem(my_tp // 2, 2), pieces - 1)
-    my_layer = my_piece // tiles
 
     def is_me(device):
         return me == device[0] * ntp + device[1]
 
+    hub = (0, ntp - 1)
+    is_hub = is_me(hub)
+    my_piece = jnp.int32(0)
+    for j in range(1, pieces):
+        my_piece = jnp.where(is_me(owners[j]), j, my_piece)
+    owning = (my_piece > 0) | is_me(owners[0])
+    my_layer = my_piece // tiles
+
     def each_other(act):
         for device in devices:
-            if device in owners:
+            if device in owners or device == hub:
 
                 @pl.when(jnp.logical_not(is_me(device)))
                 def _():
@@ -100,43 +103,69 @@
         pltpu.make_async_copy(weights, w_buf, wm_sem.at[0]),
         pltpu.make_async_copy(momentum, m_buf, wm_sem.at[1]),
     ]
-    for load in state_loads:
-        load.start()
 
     barrier = pltpu.get_barrier_semaphore()
-    dp_peers = [(lax.rem(my_dp + k, ndp), my_tp) for k in range(1, ndp)]
-    tp_peers = [(my_dp, lax.rem(my_tp + k, ntp)) for k in range(1, ntp)]
-    for peer in dp_peers + tp_peers:
-        pl.semaphore_signal(barrier, inc=1, device_id=peer, device_id_type=MESH)
-
-    @pl.when(owning)
-    def _():
-        each_other(lambda device: pl.semaphore_signal(barrier, inc=1, device_id=device, device_id_type=MESH))
+    for k in range(1, ndp):
+
+        @pl.when(k > my_dp)
+        def _():
+            pl.semaphore_signal(barrier, inc=1, device_id=(k, my_tp), device_id_type=MESH)
+
+    @pl.when(jnp.logical_not(is_hub))
+    def _():
+        pl.semaphore_signal(barrier, inc=1, device_id=hub, device_id_type=MESH)
+
+    @pl.when(my_dp > 0)
+    def _():
+        pl.semaphore_wait(barrier, my_dp)
+
+    for k in range(ndp - 1):
+
+        @pl.when(k < my_dp)
+        def _():
+            pl.semaphore_signal(ready.at[my_dp], inc=1, device_id=(k, my_tp), device_id_type=MESH)
 
     grams[my_tp] = jnp.zeros(grams.shape[1:], jnp.float32)
 
-    def left_copy(q, peer):
+    def left_copy(q, k):
         return pltpu.make_async_remote_copy(
             src_ref=lefts.at[q, my_dp], dst_ref=lefts.at[q, my_dp],
             send_sem=left_send, recv_sem=left_recv.at[q],
-            device_id=peer, device_id_type=MESH,
+            device_id=(k, my_tp), device_id_type=MESH,
         )
 
     basis_load.wait()
-    for load in loads:
-        load.wait()
-    own_left = [
-        lax.dot_general(
-            b_buf[l].astype(jnp.bfloat16), g_buf[l], (((1,), (1,)), ((), ())), preferred_element_type=jnp.float32
-        )
-        for l in range(layers)
-    ]
     for q in range(layers // 2):
-        lefts[q, my_dp] = pack(own_left[2 * q:2 * q + 2])
-    pl.semaphore_wait(barrier, ndp - 1 + ntp - 1 + pieces - jnp.where(owning, 1, 0))
-    for q in range(layers // 2):
-        for peer in dp_peers:
-            left_copy(q, peer).start()
+        pair = (2 * q, 2 * q + 1)
+        for l in pair:
+            loads[l].wait()
+        lefts[q, my_dp] = pack([
+            lax.dot_general(
+                b_buf[l].astype(jnp.bfloat16), g_buf[l], (((1,), (1,)), ((), ())), preferred_element_type=jnp.float32
+            )
+            for l in pair
+        ])
+        for k in range(ndp - 1):
+
+            @pl.when(k < my_dp)
+            def _():
+                left_copy(q, k).start()
+    for load in state_loads:
+        load.start()
+    for k in range(1, ndp):
+
+        @pl.when(k > my_dp)
+        def _():
+            pl.semaphore_wait(ready.at[k], 1)
+            for q in range(layers // 2):
+                left_copy(q, k).start()
+
+    @pl.when(is_hub)
+    def _():
+        pl.semaphore_wait(barrier, n - 1)
+        each_other(lambda device: pl.semaphore_signal(go, inc=1, device_id=device, device_id_type=MESH))
+
+    tp_peers = [(my_dp, lax.rem(my_tp + k, ntp)) for k in range(1, ntp)]
 
     def part_copy(j):
         return pltpu.make_async_remote_copy(
@@ -157,6 +186,12 @@
             right = jnp.dot(left.astype(jnp.bfloat16), g_buf[l], preferred_element_type=jnp.float32)
             for t in range(tiles):
                 rights[l * tiles + t] = right[:, t * LANES:(t + 1) * LANES]
+        if q == 0:
+
+            @pl.when(jnp.logical_not(is_hub))
+            def _():
+                pl.semaphore_wait(go, 1)
+
         for j in range(2 * q * tiles, (2 * q + 2) * tiles):
 
             @pl.when(jnp.logical_not(is_me(owners[j])))
@@ -337,6 +372,8 @@
                 pltpu.SemaphoreType.DMA,
                 pltpu.SemaphoreType.DMA,
                 pltpu.SemaphoreType.DMA((layers,)),
+                pltpu.SemaphoreType.REGULAR((ndp,)),
+                pltpu.SemaphoreType.REGULAR,
             ],
             compiler_params=pltpu.CompilerParams(
                 collective_id=0, has_side_effects=True, vmem_limit_bytes=24 * 1024 * 1024

time: 27.6 us -> 25.8 us (0.935)
  Pallas kernels: 26.9 us -> 25 us
    pallas_call x1, Pallas kernels: 25.9 us -> 24.1 us  [on_device(): pl.pallas_call(functools.partial(kernel, ndp, ntp), out_shape=(jax.ShapeD...]
where the time goes in v3:
time: 25.8 us; the launch traced here: 25.6 us
  Pallas kernels  25 us (97%)
  between operations  0.64 us (2%)
    pallas_call x1, Pallas kernels, on_device(): pl.pallas_call(functools.partial(kernel, ndp, ntp), out_shape=(jax.ShapeD...  24.1 us
    pallas_call x1, Pallas kernels, on_device(): pl.pallas_call(writer, out_shape=tuple((jax.ShapeDtypeStruct(x.shape, x.d...  0.94 us

profile of v3, /device:TPU:1, one launch (start us, length us, event | category | flops | bytes accessed | tf_op | source)
XLA Modules:
  0.0 25.6 jit_solution(16577661084998709521)
XLA Ops:
  0.6 24.1 %shard_map.67 = (f32[4,192,96]{2,1,0:T(8,128)S(1)}, f32[4,8,768]{2,1,0:T(8,128)S(1)}, f32[4,192,96]{2,1,0:T(8,128)S(1)}) custom-call(bf16[4,192,768]{2,1,0:T(8,128)(2,1)} %bitcast.3, f32[4,8,768]{2,1,0:T(8,128)} %bitcast.4, f32[4,192,96]{2,1,0:T(8,128)} %weights.1, f32[4,192,96]{2,1,0:T(8,128)} %momentum.1), custom_call_target="tpu_custom_call" | custom-call | tf_op jit(solution)/shard_map/pallas_call | solution.py:340
  24.7 0.9 %shard_map.68 = (f32[4,192,96]{2,1,0:T(8,128)}, f32[4,8,768]{2,1,0:T(8,128)}, f32[4,192,96]{2,1,0:T(8,128)}) custom-call(f32[4,192,96]{2,1,0:T(8,128)S(1)} %get-tuple-element.9.refs_0_, f32[4,8,768]{2,1,0:T(8,128)S(1)} %get-tuple-element.10.refs_1_, f32[4,192,96]{2,1,0:T(8,128)S(1)} %get-tuple-element.11.refs_2_), custom_call_target="tpu_custom_call" | custom-call | tf_op jit(solution)/shard_map/pallas_call | solution.py:385

commit v4 on v3

--- a/solution.py
+++ b/solution.py
@@ -52,7 +52,7 @@
     out_weights, out_basis, out_momentum,
     b_buf, g_buf, w_buf, m_buf, lefts, grams, rights, parts, full, y_buf,
     g_sem, wm_sem, left_send, left_recv, gram_send, gram_recv, part_send, part_recv, full_send, full_recv,
-    ready, go,
+    go,
 ):
     layers, rows, width = grads.shape
     rank = basis.shape[1]
@@ -76,7 +76,7 @@
     def is_me(device):
         return me == device[0] * ntp + device[1]
 
-    hub = (0, ntp - 1)
+    hub = (ndp - 2, ntp - 1)
     is_hub = is_me(hub)
     my_piece = jnp.int32(0)
     for j in range(1, pieces):
@@ -105,33 +105,21 @@
     ]
 
     barrier = pltpu.get_barrier_semaphore()
-    for k in range(1, ndp):
-
-        @pl.when(k > my_dp)
-        def _():
-            pl.semaphore_signal(barrier, inc=1, device_id=(k, my_tp), device_id_type=MESH)
-
-    @pl.when(jnp.logical_not(is_hub))
+    dp_peers = [(lax.rem(my_dp + k, ndp), my_tp) for k in range(1, ndp)]
+    for peer in dp_peers:
+        pl.semaphore_signal(barrier, inc=1, device_id=peer, device_id_type=MESH)
+
+    @pl.when(my_tp != hub[1])
     def _():
         pl.semaphore_signal(barrier, inc=1, device_id=hub, device_id_type=MESH)
 
-    @pl.when(my_dp > 0)
-    def _():
-        pl.semaphore_wait(barrier, my_dp)
-
-    for k in range(ndp - 1):
-
-        @pl.when(k < my_dp)
-        def _():
-            pl.semaphore_signal(ready.at[my_dp], inc=1, device_id=(k, my_tp), device_id_type=MESH)
-
     grams[my_tp] = jnp.zeros(grams.shape[1:], jnp.float32)
 
-    def left_copy(q, k):
+    def left_copy(q, peer):
         return pltpu.make_async_remote_copy(
             src_ref=lefts.at[q, my_dp], dst_ref=lefts.at[q, my_dp],
             send_sem=left_send, recv_sem=left_recv.at[q],
-            device_id=(k, my_tp), device_id_type=MESH,
+            device_id=peer, device_id_type=MESH,
         )
 
     basis_load.wait()
@@ -145,24 +133,15 @@
             )
             for l in pair
         ])
-        for k in range(ndp - 1):
-
-            @pl.when(k < my_dp)
-            def _():
-                left_copy(q, k).start()
     for load in state_loads:
         load.start()
-    for k in range(1, ndp):
-
-        @pl.when(k > my_dp)
-        def _():
-            pl.semaphore_wait(ready.at[k], 1)
-            for q in range(layers // 2):
-                left_copy(q, k).start()
+    pl.semaphore_wait(barrier, jnp.where(is_hub, n - 1, ndp - 1))
+    for q in range(layers // 2):
+        for peer in dp_peers:
+            left_copy(q, peer).start()
 
     @pl.when(is_hub)
     def _():
-        pl.semaphore_wait(barrier, n - 1)
         each_other(lambda device: pl.semaphore_signal(go, inc=1, device_id=device, device_id_type=MESH))
 
     tp_peers = [(my_dp, lax.rem(my_tp + k, ntp)) for k in range(1, ntp)]
@@ -372,7 +351,6 @@
                 pltpu.SemaphoreType.DMA,
                 pltpu.SemaphoreType.DMA,
                 pltpu.SemaphoreType.DMA((layers,)),
-                pltpu.SemaphoreType.REGULAR((ndp,)),
                 pltpu.SemaphoreType.REGULAR,
             ],
             compiler_params=pltpu.CompilerParams(

time: 25.8 us -> 25.1 us (0.973)
  Pallas kernels: 25 us -> 24.3 us
    pallas_call x1, Pallas kernels: 24.1 us -> 23.4 us  [on_device(): pl.pallas_call(functools.partial(kernel, ndp, ntp), out_shape=(jax.ShapeD...]
where the time goes in v4:
time: 25.1 us; the launch traced here: 25 us
  Pallas kernels  24.3 us (97%)
  between operations  0.64 us (3%)
    pallas_call x1, Pallas kernels, on_device(): pl.pallas_call(functools.partial(kernel, ndp, ntp), out_shape=(jax.ShapeD...  23.4 us
    pallas_call x1, Pallas kernels, on_device(): pl.pallas_call(writer, out_shape=tuple((jax.ShapeDtypeStruct(x.shape, x.d...  0.94 us

profile of v4, /device:TPU:1, one launch (start us, length us, event | category | flops | bytes accessed | tf_op | source)
XLA Modules:
  0.0 25.0 jit_solution(404397822609022446)
XLA Ops:
  0.6 23.4 %shard_map.67 = (f32[4,192,96]{2,1,0:T(8,128)S(1)}, f32[4,8,768]{2,1,0:T(8,128)S(1)}, f32[4,192,96]{2,1,0:T(8,128)S(1)}) custom-call(bf16[4,192,768]{2,1,0:T(8,128)(2,1)} %bitcast.3, f32[4,8,768]{2,1,0:T(8,128)} %bitcast.4, f32[4,192,96]{2,1,0:T(8,128)} %weights.1, f32[4,192,96]{2,1,0:T(8,128)} %momentum.1), custom_call_target="tpu_custom_call" | custom-call | tf_op jit(solution)/shard_map/pallas_call | solution.py:319
  24.0 0.9 %shard_map.68 = (f32[4,192,96]{2,1,0:T(8,128)}, f32[4,8,768]{2,1,0:T(8,128)}, f32[4,192,96]{2,1,0:T(8,128)}) custom-call(f32[4,192,96]{2,1,0:T(8,128)S(1)} %get-tuple-element.9.refs_0_, f32[4,8,768]{2,1,0:T(8,128)S(1)} %get-tuple-element.10.refs_1_, f32[4,192,96]{2,1,0:T(8,128)S(1)} %get-tuple-element.11.refs_2_), custom_call_target="tpu_custom_call" | custom-call | tf_op jit(solution)/shard_map/pallas_call | solution.py:363

commit v5 on v4

--- a/solution.py
+++ b/solution.py
@@ -36,9 +36,12 @@
     ]
 
 
+OWNERS = [(0, 0, 0, 1), (0, 0, 3, 1), (3, 0, 0, 1), (2, 0, 0, 1), (1, 0, 0, 1), (0, 1, 0, 1), (0, 0, 1, 1), (0, 0, 2, 1), (0, 3, 0, 1), (3, 0, 3, 1), (2, 0, 3, 1), (0, 1, 3, 1), (1, 0, 3, 1), (0, 3, 3, 1), (0, 2, 0, 1), (3, 3, 0, 1), (2, 1, 0, 1), (1, 1, 0, 1), (3, 1, 0, 1), (3, 0, 1, 1), (3, 0, 2, 1), (1, 0, 1, 1), (2, 0, 1, 1), (1, 0, 2, 1)]
+
+
 def owner_place(j):
-    x_hi, y, z = j % 2, j // 2 % 4, j // 8
-    return y * 2 + (y + z) % 2, z * 4 + x_hi * 2 + 1
+    x, y, z, core = OWNERS[j]
+    return y * 2 + x % 2, z * 4 + x // 2 * 2 + core
 
 
 def start_order(device):

time: 25.1 us -> 24.1 us (0.960)
  Pallas kernels: 24.3 us -> 23.3 us
    pallas_call x1, Pallas kernels: 23.4 us -> 22.4 us  [on_device(): pl.pallas_call(functools.partial(kernel, ndp, ntp), out_shape=(jax.ShapeD...]
where the time goes in v5:
time: 24.1 us; the launch traced here: 23.9 us
  Pallas kernels  23.3 us (97%)
  between operations  0.64 us (3%)
    pallas_call x1, Pallas kernels, on_device(): pl.pallas_call(functools.partial(kernel, ndp, ntp), out_shape=(jax.ShapeD...  22.4 us
    pallas_call x1, Pallas kernels, on_device(): pl.pallas_call(writer, out_shape=tuple((jax.ShapeDtypeStruct(x.shape, x.d...  0.94 us

profile of v5, /device:TPU:1, one launch (start us, length us, event | category | flops | bytes accessed | tf_op | source)
XLA Modules:
  0.0 23.9 jit_solution(13761121484695446373)
XLA Ops:
  0.6 22.4 %shard_map.67 = (f32[4,192,96]{2,1,0:T(8,128)S(1)}, f32[4,8,768]{2,1,0:T(8,128)S(1)}, f32[4,192,96]{2,1,0:T(8,128)S(1)}) custom-call(bf16[4,192,768]{2,1,0:T(8,128)(2,1)} %bitcast.3, f32[4,8,768]{2,1,0:T(8,128)} %bitcast.4, f32[4,192,96]{2,1,0:T(8,128)} %weights.1, f32[4,192,96]{2,1,0:T(8,128)} %momentum.1), custom_call_target="tpu_custom_call" | custom-call | tf_op jit(solution)/shard_map/pallas_call | solution.py:322
  23.0 0.9 %shard_map.68 = (f32[4,192,96]{2,1,0:T(8,128)}, f32[4,8,768]{2,1,0:T(8,128)}, f32[4,192,96]{2,1,0:T(8,128)}) custom-call(f32[4,192,96]{2,1,0:T(8,128)S(1)} %get-tuple-element.9.refs_0_, f32[4,8,768]{2,1,0:T(8,128)S(1)} %get-tuple-element.10.refs_1_, f32[4,192,96]{2,1,0:T(8,128)S(1)} %get-tuple-element.11.refs_2_), custom_call_target="tpu_custom_call" | custom-call | tf_op jit(solution)/shard_map/pallas_call | solution.py:366

commit v6 on v5

--- a/solution.py
+++ b/solution.py
@@ -53,9 +53,8 @@
 def kernel(
     ndp, ntp, grads, basis, weights, momentum,
     out_weights, out_basis, out_momentum,
-    b_buf, g_buf, w_buf, m_buf, lefts, grams, rights, parts, full, y_buf,
-    g_sem, wm_sem, left_send, left_recv, gram_send, gram_recv, part_send, part_recv, full_send, full_recv,
-    go,
+    b_buf, g_buf, state, lefts, grams, rights, parts, full, y_buf,
+    g_sem, b_sem, state_sem, send, left_recv, gram_recv, part_recv, full_send, full_recv, go,
 ):
     layers, rows, width = grads.shape
     rank = basis.shape[1]
@@ -85,7 +84,6 @@
     for j in range(1, pieces):
         my_piece = jnp.where(is_me(owners[j]), j, my_piece)
     owning = (my_piece > 0) | is_me(owners[0])
-    my_layer = my_piece // tiles
 
     def each_other(act):
         for device in devices:
@@ -97,18 +95,25 @@
             else:
                 act(device)
 
-    basis_load = pltpu.make_async_copy(basis, b_buf, wm_sem.at[2])
+    basis_load = pltpu.make_async_copy(basis, b_buf, b_sem)
+    loads = [
+        pltpu.make_async_copy(grads.at[l], g_buf.at[l], g_sem.at[l // 2]) for l in range(layers)
+    ]
+    for load in loads[:2]:
+        load.start()
     basis_load.start()
-    loads = [pltpu.make_async_copy(grads.at[l], g_buf.at[l], g_sem.at[l]) for l in range(layers)]
-    for load in loads:
+    for load in loads[2:]:
         load.start()
     state_loads = [
-        pltpu.make_async_copy(weights, w_buf, wm_sem.at[0]),
-        pltpu.make_async_copy(momentum, m_buf, wm_sem.at[1]),
+        pltpu.make_async_copy(weights, state.at[0], state_sem),
+        pltpu.make_async_copy(momentum, state.at[1], state_sem),
     ]
 
     barrier = pltpu.get_barrier_semaphore()
-    dp_peers = [(lax.rem(my_dp + k, ndp), my_tp) for k in range(1, ndp)]
+    dp_peers = [
+        (lax.rem(my_dp // 2 + dy, ndp // 2) * 2 + lax.rem(my_dp + dx, 2), my_tp)
+        for dy, dx in ((2, 1), (1, 1), (3, 1), (2, 0), (1, 0), (3, 0), (0, 1))
+    ]
     for peer in dp_peers:
         pl.semaphore_signal(barrier, inc=1, device_id=peer, device_id_type=MESH)
 
@@ -121,19 +126,19 @@
     def left_copy(q, peer):
         return pltpu.make_async_remote_copy(
             src_ref=lefts.at[q, my_dp], dst_ref=lefts.at[q, my_dp],
-            send_sem=left_send, recv_sem=left_recv.at[q],
+            send_sem=send, recv_sem=left_recv.at[q],
             device_id=peer, device_id_type=MESH,
         )
 
     basis_load.wait()
     for q in range(layers // 2):
         pair = (2 * q, 2 * q + 1)
-        for l in pair:
-            loads[l].wait()
+        loaded = g_buf.at[pl.ds(2 * q, 2)]
+        pltpu.make_async_copy(loaded, loaded, g_sem.at[q]).wait()
         lefts[q, my_dp] = pack([
             lax.dot_general(
-                b_buf[l].astype(jnp.bfloat16), g_buf[l], (((1,), (1,)), ((), ())), preferred_element_type=jnp.float32
-            )
+                g_buf[l], b_buf[l].astype(jnp.bfloat16), (((1,), (1,)), ((), ())), preferred_element_type=jnp.float32
+            ).T
             for l in pair
         ])
     for load in state_loads:
@@ -152,7 +157,7 @@
     def part_copy(j):
         return pltpu.make_async_remote_copy(
             src_ref=rights.at[j], dst_ref=parts.at[me],
-            send_sem=part_send, recv_sem=part_recv,
+            send_sem=send, recv_sem=part_recv,
             device_id=owners[j], device_id_type=MESH,
         )
 
@@ -194,7 +199,7 @@
     def gram_copy(peer):
         return pltpu.make_async_remote_copy(
             src_ref=grams.at[my_tp], dst_ref=grams.at[my_tp],
-            send_sem=gram_send, recv_sem=gram_recv,
+            send_sem=send, recv_sem=gram_recv,
             device_id=peer, device_id_type=MESH,
         )
 
@@ -204,7 +209,7 @@
     def full_copy(device):
         return pltpu.make_async_remote_copy(
             src_ref=full.at[my_piece], dst_ref=full.at[my_piece],
-            send_sem=full_send, recv_sem=full_recv.at[my_layer],
+            send_sem=full_send, recv_sem=full_recv,
             device_id=device, device_id_type=MESH,
         )
 
@@ -248,54 +253,49 @@
         high, mid, low = split3(systems[l][1] / ndp)
         y = jnp.concatenate([high, high, high, mid, mid, low], axis=0)
         y_buf[l] = y.T.astype(jnp.bfloat16)
-    for load in state_loads:
-        load.wait()
+    pltpu.make_async_copy(state, state, state_sem).wait()
 
     start = first_tile(my_dp, jnp.minimum)
     shift = lax.rem(span * LANES - (my_dp * columns - start * LANES), span * LANES)
 
-    def wait_full(l, count):
-        landed = full.at[pl.ds(l * tiles, count)]
-        pltpu.make_async_copy(landed, landed, full_recv.at[l]).wait()
+    def wait_full(count):
+        landed = full.at[pl.ds(0, count)]
+        pltpu.make_async_copy(landed, landed, full_recv).wait()
+
+    @pl.when(owning)
+    def _():
+        wait_full(pieces - 1)
+
+    @pl.when(jnp.logical_not(owning))
+    def _():
+        wait_full(pieces)
 
     for l in range(layers):
-        own_layer = owning & (my_layer == l)
-
-        @pl.when(own_layer)
-        def _():
-            wait_full(l, tiles - 1)
-
-        @pl.when(jnp.logical_not(own_layer))
-        def _():
-            wait_full(l, tiles)
-
-        near = jnp.concatenate([full[l * tiles + start + i] for i in range(span)], axis=1)
+        near = jnp.concatenate([full[l * tiles + start + b] for b in range(span)], axis=1)
         own = pltpu.roll(near, shift, 1)[:, :columns]
         high, mid, low = split3(own)
         own = jnp.concatenate([high, mid, low, high, mid, high], axis=0).astype(jnp.bfloat16)
         change = jnp.dot(y_buf[l], own, preferred_element_type=jnp.float32)
-        moved = 0.9 * m_buf[l] + change
+        moved = 0.9 * state[1, l] + change
         out_momentum[l] = moved
-        out_weights[l] = w_buf[l] - 0.02 * moved
+        out_weights[l] = state[0, l] - 0.02 * moved
         right = jnp.concatenate([full[l * tiles + t] for t in range(tiles)], axis=1)
         out_basis[l] = right * lax.rsqrt(jnp.mean(right * right) + 1e-12)
 
-    for q in range(layers // 2):
-        sent = lefts.at[q, pl.ds(0, ndp - 1)]
-        pltpu.make_async_copy(sent, sent, left_send).wait()
-    pltpu.make_async_copy(landed_grams, landed_grams, gram_send).wait()
+    tile_sends = layers // 2 * (ndp - 1) * lefts.shape[3] // LANES + ntp - 1 + pieces
+
+    def wait_sent(count, sem):
+        sent = parts.at[pl.ds(0, count)]
+        pltpu.make_async_copy(sent, sent, sem).wait()
 
     @pl.when(owning)
     def _():
-        sent = rights.at[pl.ds(0, pieces - 1)]
-        pltpu.make_async_copy(sent, sent, part_send).wait()
-        sent = parts.at[pl.ds(0, n - 1)]
-        pltpu.make_async_copy(sent, sent, full_send).wait()
+        wait_sent(tile_sends - 1, send)
+        wait_sent(n - 1, full_send)
 
     @pl.when(jnp.logical_not(owning))
     def _():
-        sent = rights.at[pl.ds(0, pieces)]
-        pltpu.make_async_copy(sent, sent, part_send).wait()
+        wait_sent(tile_sends, send)
 
 
 def writer(*refs):
@@ -336,24 +336,22 @@
             scratch_shapes=[
                 pltpu.VMEM((layers, rank, width), f32),
                 pltpu.VMEM((layers, rows, width), jnp.bfloat16),
-                pltpu.VMEM((layers, rows, columns), f32),
-                pltpu.VMEM((layers, rows, columns), f32),
+                pltpu.VMEM((2, layers, rows, columns), f32),
                 pltpu.VMEM((layers // 2, ndp, rank, 2 * rows), f32),
                 pltpu.VMEM((ntp, rank, LANES), f32),
                 pltpu.VMEM((pieces, rank, LANES), f32),
                 pltpu.VMEM((n, rank, LANES), f32),
                 pltpu.VMEM((pieces, rank, LANES), f32),
                 pltpu.VMEM((layers, rows, 6 * rank), jnp.bfloat16),
-                pltpu.SemaphoreType.DMA((layers,)),
-                pltpu.SemaphoreType.DMA((3,)),
-                pltpu.SemaphoreType.DMA,
                 pltpu.SemaphoreType.DMA((layers // 2,)),
                 pltpu.SemaphoreType.DMA,
                 pltpu.SemaphoreType.DMA,
                 pltpu.SemaphoreType.DMA,
-                pltpu.SemaphoreType.DMA,
-                pltpu.SemaphoreType.DMA,
-                pltpu.SemaphoreType.DMA((layers,)),
+                pltpu.SemaphoreType.DMA((layers // 2,)),
+                pltpu.SemaphoreType.DMA,
+                pltpu.SemaphoreType.DMA,
+                pltpu.SemaphoreType.DMA,
+                pltpu.SemaphoreType.DMA,
                 pltpu.SemaphoreType.REGULAR,
             ],
             compiler_params=pltpu.CompilerParams(

time: 24.1 us -> 23.6 us (0.979)
  Pallas kernels: 23.3 us -> 22.8 us
    pallas_call x1, Pallas kernels: 22.4 us -> 21.9 us  [on_device(): pl.pallas_call(functools.partial(kernel, ndp, ntp), out_shape=(jax.ShapeD...]
where the time goes in v6:
time: 23.6 us; the launch traced here: 23.5 us
  Pallas kernels  22.8 us (97%)
  between operations  0.64 us (3%)
    pallas_call x1, Pallas kernels, on_device(): pl.pallas_call(functools.partial(kernel, ndp, ntp), out_shape=(jax.ShapeD...  21.9 us
    pallas_call x1, Pallas kernels, on_device(): pl.pallas_call(writer, out_shape=tuple((jax.ShapeDtypeStruct(x.shape, x.d...  0.94 us

profile of v6, /device:TPU:1, one launch (start us, length us, event | category | flops | bytes accessed | tf_op | source)
XLA Modules:
  0.0 23.5 jit_solution(15300075094737260920)
XLA Ops:
  0.6 21.9 %shard_map.67 = (f32[4,192,96]{2,1,0:T(8,128)S(1)}, f32[4,8,768]{2,1,0:T(8,128)S(1)}, f32[4,192,96]{2,1,0:T(8,128)S(1)}) custom-call(bf16[4,192,768]{2,1,0:T(8,128)(2,1)} %bitcast.3, f32[4,8,768]{2,1,0:T(8,128)} %bitcast.4, f32[4,192,96]{2,1,0:T(8,128)} %weights.1, f32[4,192,96]{2,1,0:T(8,128)} %momentum.1), custom_call_target="tpu_custom_call" | custom-call | tf_op jit(solution)/shard_map/pallas_call | solution.py:322
  22.5 0.9 %shard_map.68 = (f32[4,192,96]{2,1,0:T(8,128)}, f32[4,8,768]{2,1,0:T(8,128)}, f32[4,192,96]{2,1,0:T(8,128)}) custom-call(f32[4,192,96]{2,1,0:T(8,128)S(1)} %get-tuple-element.9.refs_0_, f32[4,8,768]{2,1,0:T(8,128)S(1)} %get-tuple-element.10.refs_1_, f32[4,192,96]{2,1,0:T(8,128)S(1)} %get-tuple-element.11.refs_2_), custom_call_target="tpu_custom_call" | custom-call | tf_op jit(solution)/shard_map/pallas_call | solution.py:364

commit v7 on v6

--- a/solution.py
+++ b/solution.py
@@ -36,7 +36,14 @@
     ]
 
 
-OWNERS = [(0, 0, 0, 1), (0, 0, 3, 1), (3, 0, 0, 1), (2, 0, 0, 1), (1, 0, 0, 1), (0, 1, 0, 1), (0, 0, 1, 1), (0, 0, 2, 1), (0, 3, 0, 1), (3, 0, 3, 1), (2, 0, 3, 1), (0, 1, 3, 1), (1, 0, 3, 1), (0, 3, 3, 1), (0, 2, 0, 1), (3, 3, 0, 1), (2, 1, 0, 1), (1, 1, 0, 1), (3, 1, 0, 1), (3, 0, 1, 1), (3, 0, 2, 1), (1, 0, 1, 1), (2, 0, 1, 1), (1, 0, 2, 1)]
+OWNERS = [
+    (0, 3, 1, 1), (0, 0, 3, 1), (3, 0, 0, 1), (2, 0, 0, 1),
+    (1, 0, 0, 1), (0, 1, 0, 1), (0, 0, 1, 1), (0, 0, 2, 1),
+    (0, 3, 0, 1), (3, 0, 3, 1), (2, 0, 3, 1), (0, 1, 3, 1),
+    (1, 0, 3, 1), (1, 1, 1, 1), (0, 2, 0, 1), (1, 1, 3, 1),
+    (0, 1, 2, 1), (1, 1, 0, 1), (3, 1, 0, 1), (3, 0, 1, 1),
+    (0, 1, 1, 1), (1, 0, 1, 1), (2, 0, 1, 1), (1, 0, 2, 1),
+]
 
 
 def owner_place(j):
@@ -99,11 +106,6 @@
     loads = [
         pltpu.make_async_copy(grads.at[l], g_buf.at[l], g_sem.at[l // 2]) for l in range(layers)
     ]
-    for load in loads[:2]:
-        load.start()
-    basis_load.start()
-    for load in loads[2:]:
-        load.start()
     state_loads = [
         pltpu.make_async_copy(weights, state.at[0], state_sem),
         pltpu.make_async_copy(momentum, state.at[1], state_sem),
@@ -116,6 +118,12 @@
     ]
     for peer in dp_peers:
         pl.semaphore_signal(barrier, inc=1, device_id=peer, device_id_type=MESH)
+
+    for load in loads[:2]:
+        load.start()
+    basis_load.start()
+    for load in loads[2:]:
+        load.start()
 
     @pl.when(my_tp != hub[1])
     def _():

time: 23.6 us -> 23.5 us (level)
  no operation moved by 1% of the time
where the time goes in v7:
time: 23.5 us; the launch traced here: 23.3 us
  Pallas kernels  22.7 us (97%)
  between operations  0.64 us (3%)
    pallas_call x1, Pallas kernels, on_device(): pl.pallas_call(functools.partial(kernel, ndp, ntp), out_shape=(jax.ShapeD...  21.7 us
    pallas_call x1, Pallas kernels, on_device(): pl.pallas_call(writer, out_shape=tuple((jax.ShapeDtypeStruct(x.shape, x.d...  0.94 us

profile of v7, /device:TPU:1, one launch (start us, length us, event | category | flops | bytes accessed | tf_op | source)
XLA Modules:
  0.0 23.3 jit_solution(15538567304668749947)
XLA Ops:
  0.6 21.7 %shard_map.67 = (f32[4,192,96]{2,1,0:T(8,128)S(1)}, f32[4,8,768]{2,1,0:T(8,128)S(1)}, f32[4,192,96]{2,1,0:T(8,128)S(1)}) custom-call(bf16[4,192,768]{2,1,0:T(8,128)(2,1)} %bitcast.3, f32[4,8,768]{2,1,0:T(8,128)} %bitcast.4, f32[4,192,96]{2,1,0:T(8,128)} %weights.1, f32[4,192,96]{2,1,0:T(8,128)} %momentum.1), custom_call_target="tpu_custom_call" | custom-call | tf_op jit(solution)/shard_map/pallas_call | solution.py:330
  22.4 0.9 %shard_map.68 = (f32[4,192,96]{2,1,0:T(8,128)}, f32[4,8,768]{2,1,0:T(8,128)}, f32[4,192,96]{2,1,0:T(8,128)}) custom-call(f32[4,192,96]{2,1,0:T(8,128)S(1)} %get-tuple-element.9.refs_0_, f32[4,8,768]{2,1,0:T(8,128)S(1)} %get-tuple-element.10.refs_1_, f32[4,192,96]{2,1,0:T(8,128)S(1)} %get-tuple-element.11.refs_2_), custom_call_target="tpu_custom_call" | custom-call | tf_op jit(solution)/shard_map/pallas_call | solution.py:372

commit v8 on v7

--- a/solution.py
+++ b/solution.py
@@ -41,7 +41,7 @@
     (1, 0, 0, 1), (0, 1, 0, 1), (0, 0, 1, 1), (0, 0, 2, 1),
     (0, 3, 0, 1), (3, 0, 3, 1), (2, 0, 3, 1), (0, 1, 3, 1),
     (1, 0, 3, 1), (1, 1, 1, 1), (0, 2, 0, 1), (1, 1, 3, 1),
-    (0, 1, 2, 1), (1, 1, 0, 1), (3, 1, 0, 1), (3, 0, 1, 1),
+    (0, 1, 2, 1), (1, 1, 0, 1), (3, 1, 3, 1), (3, 0, 1, 1),
     (0, 1, 1, 1), (1, 0, 1, 1), (2, 0, 1, 1), (1, 0, 2, 1),
 ]
 
@@ -54,7 +54,7 @@
 def start_order(device):
     dp, tp = device
     x, y, z, core = tp // 2 % 2 * 2 + dp % 2, dp // 2, tp // 4, tp % 2
-    return 10 * z + 6 * y + 4 * x + 5 * (1 - core)
+    return 12 * z + 6 * y + 4 * x + 5 * (1 - core)
 
 
 def kernel(

time: 23.5 us -> 23.5 us (level)
  no operation moved by 1% of the time
where the time goes in v8:
time: 23.5 us; the launch traced here: 23.3 us
  Pallas kernels  22.7 us (97%)
  between operations  0.64 us (3%)
    pallas_call x1, Pallas kernels, on_device(): pl.pallas_call(functools.partial(kernel, ndp, ntp), out_shape=(jax.ShapeD...  21.7 us
    pallas_call x1, Pallas kernels, on_device(): pl.pallas_call(writer, out_shape=tuple((jax.ShapeDtypeStruct(x.shape, x.d...  0.94 us

profile of v8, /device:TPU:1, one launch (start us, length us, event | category | flops | bytes accessed | tf_op | source)
XLA Modules:
  0.0 23.3 jit_solution(7294206775732123859)
XLA Ops:
  0.6 21.7 %shard_map.67 = (f32[4,192,96]{2,1,0:T(8,128)S(1)}, f32[4,8,768]{2,1,0:T(8,128)S(1)}, f32[4,192,96]{2,1,0:T(8,128)S(1)}) custom-call(bf16[4,192,768]{2,1,0:T(8,128)(2,1)} %bitcast.3, f32[4,8,768]{2,1,0:T(8,128)} %bitcast.4, f32[4,192,96]{2,1,0:T(8,128)} %weights.1, f32[4,192,96]{2,1,0:T(8,128)} %momentum.1), custom_call_target="tpu_custom_call" | custom-call | tf_op jit(solution)/shard_map/pallas_call | solution.py:330
  22.4 0.9 %shard_map.68 = (f32[4,192,96]{2,1,0:T(8,128)}, f32[4,8,768]{2,1,0:T(8,128)}, f32[4,192,96]{2,1,0:T(8,128)}) custom-call(f32[4,192,96]{2,1,0:T(8,128)S(1)} %get-tuple-element.9.refs_0_, f32[4,8,768]{2,1,0:T(8,128)S(1)} %get-tuple-element.10.refs_1_, f32[4,192,96]{2,1,0:T(8,128)S(1)} %get-tuple-element.11.refs_2_), custom_call_target="tpu_custom_call" | custom-call | tf_op jit(solution)/shard_map/pallas_call | solution.py:372

commit v9 on v8

--- a/solution.py
+++ b/solution.py
@@ -145,8 +145,8 @@
         pltpu.make_async_copy(loaded, loaded, g_sem.at[q]).wait()
         lefts[q, my_dp] = pack([
             lax.dot_general(
-                g_buf[l], b_buf[l].astype(jnp.bfloat16), (((1,), (1,)), ((), ())), preferred_element_type=jnp.float32
-            ).T
+                b_buf[l].astype(jnp.bfloat16), g_buf[l], (((1,), (1,)), ((), ())), preferred_element_type=jnp.float32
+            )
             for l in pair
         ])
     for load in state_loads:

time: 23.5 us -> 23.5 us (level)
  no operation moved by 1% of the time
where the time goes in v9:
time: 23.5 us; the launch traced here: 23.3 us
  Pallas kernels  22.7 us (97%)
  between operations  0.64 us (3%)
    pallas_call x1, Pallas kernels, on_device(): pl.pallas_call(functools.partial(kernel, ndp, ntp), out_shape=(jax.ShapeD...  21.7 us
    pallas_call x1, Pallas kernels, on_device(): pl.pallas_call(writer, out_shape=tuple((jax.ShapeDtypeStruct(x.shape, x.d...  0.94 us

profile of v9, /device:TPU:1, one launch (start us, length us, event | category | flops | bytes accessed | tf_op | source)
XLA Modules:
  0.0 23.3 jit_solution(5669714581518939473)
XLA Ops:
  0.6 21.7 %shard_map.67 = (f32[4,192,96]{2,1,0:T(8,128)S(1)}, f32[4,8,768]{2,1,0:T(8,128)S(1)}, f32[4,192,96]{2,1,0:T(8,128)S(1)}) custom-call(bf16[4,192,768]{2,1,0:T(8,128)(2,1)} %bitcast.3, f32[4,8,768]{2,1,0:T(8,128)} %bitcast.4, f32[4,192,96]{2,1,0:T(8,128)} %weights.1, f32[4,192,96]{2,1,0:T(8,128)} %momentum.1), custom_call_target="tpu_custom_call" | custom-call | tf_op jit(solution)/shard_map/pallas_call | solution.py:330
  22.4 0.9 %shard_map.68 = (f32[4,192,96]{2,1,0:T(8,128)}, f32[4,8,768]{2,1,0:T(8,128)}, f32[4,192,96]{2,1,0:T(8,128)}) custom-call(f32[4,192,96]{2,1,0:T(8,128)S(1)} %get-tuple-element.9.refs_0_, f32[4,8,768]{2,1,0:T(8,128)S(1)} %get-tuple-element.10.refs_1_, f32[4,192,96]{2,1,0:T(8,128)S(1)} %get-tuple-element.11.refs_2_), custom_call_target="tpu_custom_call" | custom-call | tf_op jit(solution)/shard_map/pallas_call | solution.py:372

commit v10 on v9

--- a/solution.py
+++ b/solution.py
@@ -149,12 +149,12 @@
             )
             for l in pair
         ])
-    for load in state_loads:
-        load.start()
     pl.semaphore_wait(barrier, jnp.where(is_hub, n - 1, ndp - 1))
     for q in range(layers // 2):
         for peer in dp_peers:
             left_copy(q, peer).start()
+    for load in state_loads:
+        load.start()
 
     @pl.when(is_hub)
     def _():

time: 23.5 us -> 23.5 us (level)
  no operation moved by 1% of the time
where the time goes in v10:
time: 23.5 us; the launch traced here: 23.3 us
  Pallas kernels  22.7 us (97%)
  between operations  0.64 us (3%)
    pallas_call x1, Pallas kernels, on_device(): pl.pallas_call(functools.partial(kernel, ndp, ntp), out_shape=(jax.ShapeD...  21.7 us
    pallas_call x1, Pallas kernels, on_device(): pl.pallas_call(writer, out_shape=tuple((jax.ShapeDtypeStruct(x.shape, x.d...  0.94 us

profile of v10, /device:TPU:1, one launch (start us, length us, event | category | flops | bytes accessed | tf_op | source)
XLA Modules:
  0.0 23.3 jit_solution(4114831031611498336)
XLA Ops:
  0.6 21.7 %shard_map.67 = (f32[4,192,96]{2,1,0:T(8,128)S(1)}, f32[4,8,768]{2,1,0:T(8,128)S(1)}, f32[4,192,96]{2,1,0:T(8,128)S(1)}) custom-call(bf16[4,192,768]{2,1,0:T(8,128)(2,1)} %bitcast.3, f32[4,8,768]{2,1,0:T(8,128)} %bitcast.4, f32[4,192,96]{2,1,0:T(8,128)} %weights.1, f32[4,192,96]{2,1,0:T(8,128)} %momentum.1), custom_call_target="tpu_custom_call" | custom-call | tf_op jit(solution)/shard_map/pallas_call | solution.py:330
  22.4 0.9 %shard_map.68 = (f32[4,192,96]{2,1,0:T(8,128)}, f32[4,8,768]{2,1,0:T(8,128)}, f32[4,192,96]{2,1,0:T(8,128)}) custom-call(f32[4,192,96]{2,1,0:T(8,128)S(1)} %get-tuple-element.9.refs_0_, f32[4,8,768]{2,1,0:T(8,128)S(1)} %get-tuple-element.10.refs_1_, f32[4,192,96]{2,1,0:T(8,128)S(1)} %get-tuple-element.11.refs_2_), custom_call_target="tpu_custom_call" | custom-call | tf_op jit(solution)/shard_map/pallas_call | solution.py:372
